TPU v7x, 256 devices: a 8x8x2 block of a 8x8x16 slice. The times are simulated.
256 devices in a mesh: groups: 2 (over z), seq: 16 (over y, core), dp: 8 (over x).
Axes of the slice: x: 8, y: 8, z: 2, core: 2. Of those that a mesh axis runs over, the one named last changes fastest.
The devices are a block of a 8x8x16 slice.
Arguments:
- resid: bfloat16 [16, 1024, 2048], P(('groups', 'dp'), 'seq'), parts along dimension 0, may hold values from -6 to 6
- queries_keys: bfloat16 [2, 16, 1024, 2048], P(None, ('groups', 'dp'), 'seq'), parts along dimension 1, may hold values from -20 to 20
- values: bfloat16 [16, 1024, 2048], P(('groups', 'dp'), 'seq'), parts along dimension 0, may hold values from -6 to 6
- doc_ids: int32 [16, 1024], P(('groups', 'dp')), parts along dimension 0, may hold values from 0 to 5, never falling along the last dimension, each value on 1 to 512 neighbouring positions
- out_weight: bfloat16 [2048, 2048], P(None, 'dp'), may hold values from -0.125 to 0.125
- norm_gain: float32 [2048], replicated, may hold values from 0.5 to 1.5
- expert_ids: int32 [16, 1024, 4], P(('groups', 'dp'), 'seq'), parts along dimension 0, may hold values from 0 to 31, all different within a row; in each aligned block of 64 rows (0 to 63, 64 to 127, ..., all dimensions but the last counted through in order) at most 10 rows name the same one
- gate_vals: float32 [16, 1024, 4], P(('groups', 'dp'), 'seq'), parts along dimension 0, may hold values from 0.05 to 0.6
- expert_gate: bfloat16 [128, 2048, 352], P(('seq', 'dp')), may hold values from -0.125 to 0.125
- expert_up: bfloat16 [128, 2048, 352], P(('seq', 'dp')), may hold values from -0.125 to 0.125
- expert_down: bfloat16 [128, 352, 2048], P(('seq', 'dp')), may hold values from -0.15625 to 0.15625
- shared_gate: bfloat16 [2048, 2816], P(None, 'dp'), may hold values from -0.125 to 0.125
- shared_up: bfloat16 [2048, 2816], P(None, 'dp'), may hold values from -0.125 to 0.125
- shared_down: bfloat16 [2816, 2048], P('dp'), may hold values from -0.109375 to 0.109375
- shared_score: bfloat16 [2048], replicated, may hold values from -0.125 to 0.125
Outputs:
- layer_out: bfloat16 [16, 1024, 2048], P(('groups', 'dp'), 'seq'), parts along dimension 0
There are 2 independent parts, one for each index of `groups`. A program takes and returns all parts, laid end to end along the dimension named above; an argument that names none is the same for every part. Nothing has to cross between parts.
Inputs may be any that keep to these rules, and one draw needn't show every extreme that they name: `doc_ids`: document numbers never fall along a sequence; each document holds 1 to 512 positions. `expert_ids`: each token names 4 different experts; among the rows of one device no expert is named more than 10 times.
All inputs are finite; a program needn't handle non-finite values.
Results may differ from a plain program's by a relative error of at most 0.01.
Values may be sent and summed in bfloat16 or wider, within the bound.
A program may use at most 128 MiB of HBM per device.

v0:
```python
import math
import jax
import jax.numpy as jnp
from jax import lax
from jax.sharding import PartitionSpec as P

HD = 128
EXPERTS = 32
TOPK = 4
SPLIT = 4
CAP = 10
norm_eps = 1e-06


def slot_numbers(routes):
    flat_routes = routes.reshape(routes.shape[:-2] + (-1,))
    matches = (flat_routes[..., None] == jnp.arange(EXPERTS, dtype=jnp.int32)).astype(jnp.int32)
    ranked = jnp.sum(matches * (jnp.cumsum(matches, axis=-2) - 1), axis=-1)
    return (flat_routes * CAP + ranked).reshape(routes.shape)


def attend_heads(queries, key_rows, value_rows, documents):
    score_scale = 1.0 / math.sqrt(queries.shape[-1])
    scores = (
        jnp.einsum("qhd,khd->hqk", queries, key_rows, preferred_element_type=jnp.float32)
        * score_scale
    )
    positions = jnp.arange(queries.shape[0], dtype=jnp.int32)
    allowed = (positions[:, None] >= positions[None, :]) & (
        documents[:, None] == documents[None, :]
    )
    scores = jnp.where(allowed[None], scores, -1e30)
    row_max = jnp.max(scores, axis=-1, keepdims=True)
    lifted = jnp.exp(scores - row_max)
    weights = (lifted / jnp.sum(lifted, axis=-1, keepdims=True)).astype(jnp.bfloat16)
    return jnp.einsum(
        "hqk,khd->qhd", weights, value_rows, preferred_element_type=jnp.float32
    ).astype(jnp.bfloat16)


def piece_block(row_block, gate_matrix, up_matrix, down_matrix):
    gate_act = jnp.einsum(
        "npcd,pdf->npcf", row_block, gate_matrix, preferred_element_type=jnp.float32
    )
    up_act = jnp.einsum("npcd,pdf->npcf", row_block, up_matrix, preferred_element_type=jnp.float32)
    hidden = (jax.nn.silu(gate_act) * up_act).astype(jnp.bfloat16)
    return jnp.einsum(
        "npcf,pfd->npcd", hidden, down_matrix, preferred_element_type=jnp.float32
    ).astype(jnp.bfloat16)


def shared_block(row_block, gate_matrix, up_matrix, down_matrix):
    gate_act = jnp.dot(row_block, gate_matrix, preferred_element_type=jnp.float32)
    up_act = jnp.dot(row_block, up_matrix, preferred_element_type=jnp.float32)
    hidden = (jax.nn.silu(gate_act) * up_act).astype(jnp.bfloat16)
    return jnp.dot(hidden, down_matrix, preferred_element_type=jnp.float32)


def body(
    resid,
    queries_keys,
    values,
    doc_ids,
    out_weight,
    norm_gain,
    expert_ids,
    gate_vals,
    expert_gate,
    expert_up,
    expert_down,
    shared_gate,
    shared_up,
    shared_down,
    shared_score,
):
    seq_count = lax.axis_size("seq")
    batch_count = lax.axis_size("dp")
    tokens = resid.shape[1]
    model_width = resid.shape[2]
    local_heads = model_width // HD // seq_count
    paired = queries_keys.reshape(2, tokens, seq_count, local_heads, HD)
    valued = values.reshape(1, tokens, seq_count, local_heads, HD)
    documents = doc_ids[0]
    pair_piece = lax.all_to_all(paired, "seq", split_axis=2, concat_axis=1, tiled=True)
    value_piece = lax.all_to_all(valued, "seq", split_axis=2, concat_axis=1, tiled=True)
    attended = attend_heads(
        pair_piece[0, :, 0], pair_piece[1, :, 0], value_piece[0, :, 0], documents
    )
    by_position = attended.reshape(seq_count, tokens, local_heads * HD)
    own_attended = lax.all_to_all(
        by_position, "seq", split_axis=0, concat_axis=2, tiled=True
    ).reshape(tokens, model_width)
    column_block = jnp.dot(
        lax.all_gather(own_attended, "dp", axis=0, tiled=True),
        out_weight,
        preferred_element_type=jnp.float32,
    ).astype(jnp.bfloat16)
    projected = lax.all_to_all(column_block, "dp", split_axis=0, concat_axis=1, tiled=True)
    residual = (resid[0].astype(jnp.float32) + projected.astype(jnp.float32)).astype(jnp.bfloat16)
    stream = residual.astype(jnp.float32)
    normed = (
        stream * lax.rsqrt(jnp.mean(stream * stream, axis=-1, keepdims=True) + norm_eps) * norm_gain
    ).astype(jnp.bfloat16)
    shared_parts = shared_block(
        lax.all_gather(normed, "dp", axis=0, tiled=True), shared_gate, shared_up, shared_down
    )
    shared_sum = lax.psum_scatter(
        shared_parts.astype(jnp.bfloat16), "dp", scatter_dimension=0, tiled=True
    ).astype(jnp.float32)
    share_weight = jax.nn.sigmoid(jnp.dot(normed, shared_score, preferred_element_type=jnp.float32))
    routes = expert_ids[0]
    route_gates = gate_vals[0]
    slot_ids = slot_numbers(routes)
    slot_range = jnp.arange(EXPERTS * CAP, dtype=jnp.int32)
    picked = jnp.sum(
        (slot_ids[None, :, :] == slot_range[:, None, None]).astype(jnp.int32), axis=-1
    ).astype(jnp.bfloat16)
    buffer = jnp.dot(picked, normed, preferred_element_type=jnp.float32).astype(jnp.bfloat16)
    outgoing = jnp.broadcast_to(
        buffer.reshape(EXPERTS, 1, CAP, model_width), (EXPERTS, SPLIT, CAP, model_width)
    )
    own_pieces = expert_gate.shape[0]
    devices = seq_count * batch_count
    incoming = lax.all_to_all(
        outgoing.reshape(EXPERTS * SPLIT, CAP, model_width),
        ("seq", "dp"),
        split_axis=0,
        concat_axis=0,
        tiled=True,
    )
    results = piece_block(
        incoming.reshape(devices, own_pieces, CAP, model_width), expert_gate, expert_up, expert_down
    )
    returned = lax.all_to_all(
        results.reshape(devices * own_pieces, CAP, model_width),
        ("seq", "dp"),
        split_axis=0,
        concat_axis=0,
        tiled=True,
    )
    expert_out = jnp.sum(
        returned.reshape(EXPERTS, SPLIT, CAP, model_width).astype(jnp.float32), axis=1
    ).reshape(EXPERTS * CAP, model_width)
    fetched = jnp.take(expert_out, slot_ids.reshape(-1), axis=0).reshape(tokens, TOPK, model_width)
    routed = jnp.sum(route_gates[..., None] * fetched, axis=1)
    layer_out = residual.astype(jnp.float32) + routed + share_weight[:, None] * shared_sum
    return layer_out.astype(jnp.bfloat16)[None]


def solution(mesh):
    placed = (
        P(("groups", "dp"), "seq", None),
        P(None, ("groups", "dp"), "seq", None),
        P(("groups", "dp"), "seq", None),
        P(("groups", "dp"), None),
        P(None, "dp"),
        P(),
        P(("groups", "dp"), "seq", None),
        P(("groups", "dp"), "seq", None),
        P(("seq", "dp"), None, None),
        P(("seq", "dp"), None, None),
        P(("seq", "dp"), None, None),
        P(None, "dp"),
        P(None, "dp"),
        P("dp", None),
        P(),
    )
    return jax.shard_map(
        body,
        mesh=mesh,
        in_specs=placed,
        out_specs=P(("groups", "dp"), "seq", None),
        check_vma=False,
    )
```

profile of v0, /device:TPU:520, one launch (start us, length us, event | category | flops | bytes accessed | tf_op | source)
XLA Modules:
  0.0 723.0 jit_solution(18105331413996864647)
XLA Ops:
  6.6 1.3 copy.92
  7.8 0.9 copy.71
  8.8 13.5 %all-to-all-start = ((bf16[2,64,16,1,128]{4,1,0,3,2:T(8,128)(2,1)}), bf16[2,64,16,1,128]{4,1,0,3,2:T(8,128)(2,1)S(1)}, u32[]{:S(2)}, u32[]{:S(2)}) async-start(bf16[2,64,16,1,128]{4,1,0,3,2:T(8,128)(2,1)} %copy.71), calls=%async_computation | async-start | bytes 1048576 | tf_op jit(solution)/shard_map/all_to_all | solution.py:84
  22.3 0.8 copy.73
  23.1 14.9 %all-to-all-done = bf16[2,64,16,1,128]{4,1,0,3,2:T(8,128)(2,1)S(1)} async-done(((bf16[2,64,16,1,128]{4,1,0,3,2:T(8,128)(2,1)}), bf16[2,64,16,1,128]{4,1,0,3,2:T(8,128)(2,1)S(1)}, u32[]{:S(2)}, u32[]{:S(2)}) %all-to-all-start) | async-done | bytes 524320 | tf_op jit(solution)/shard_map/all_to_all | solution.py:84
  38.0 4.5 all-to-all-start.1
  42.6 1.0 fusion.53
  43.6 1.9 copy-done.2
  45.6 0.6 fusion.1
  46.2 7.5 %all-to-all-done.1 = bf16[1,64,16,1,128]{4,1,3,0,2:T(8,128)(2,1)S(1)} async-done(((bf16[1,64,16,1,128]{4,1,3,0,2:T(8,128)(2,1)}), bf16[1,64,16,1,128]{4,1,3,0,2:T(8,128)(2,1)S(1)}, u32[]{:S(2)}, u32[]{:S(2)}) %all-to-all-start.1) | async-done | bytes 262176 | tf_op jit(solution)/shard_map/all_to_all | solution.py:85
  53.7 3.2 fusion.22
  56.8 14.1 %all_to_all.68 = bf16[16,64,128]{2,1,0:T(8,128)(2,1)S(1)} all-to-all(bf16[16,64,128]{2,1,0:T(8,128)(2,1)S(1)} %bitcast.167), channel_id=1, replica_groups=mesh['groups'=2,'seq'=16,'dp'=8] {'seq'}, dimensions={0} | all-to-all | bytes 524288 | tf_op jit(solution)/shard_map/all_to_all | solution.py:90
  70.9 0.2 copy.74
  71.1 0.8 copy.109
  72.2 0.6 reduce-window.6
  72.8 46.4 %all-gather.3.cloned.1.call-done = bf16[512,2048]{1,0:T(8,128)(2,1)} async-done(((bf16[64,2048]{1,0:T(8,128)(2,1)}), bf16[512,2048]{1,0:T(8,128)(2,1)}) %all-gather.3.cloned.1.call-update) | async-done | bytes 2097168 | tf_op jit(solution)/shard_map/all_gather | solution.py:94
  119.2 3.0 convolution_convert_fusion.3
  122.2 7.4 %all-to-all-start.3 = ((bf16[8,64,256]{2,1,0:T(8,128)(2,1)}), bf16[8,64,256]{2,1,0:T(8,128)(2,1)S(1)}, u32[]{:S(2)}, u32[]{:S(2)}) async-start(bf16[8,64,256]{2,1,0:T(8,128)(2,1)} %bitcast.16), calls=%async_computation.3 | async-start | bytes 524288 | tf_op jit(solution)/shard_map/all_to_all | solution.py:98
  129.5 0.2 slice_reduce_fusion
  129.7 0.1 reshape_squeeze.3
  130.2 0.1 convert_reduce_fusion.1
  130.3 4.4 all-to-all-done.3
  134.8 0.2 fusion.37
  135.0 0.7 copy-done.3
  135.7 0.1 fusion.39
  135.8 0.7 copy-done.4
  136.5 1.6 convolution_convert_fusion.2
  138.1 2.3 broadcast_in_dim.36
  140.4 1.1 broadcast_in_dim.37
  141.5 247.6 %all_to_all.69 = bf16[128,10,2048]{2,1,0:T(8,128)(2,1)} all-to-all(bf16[128,10,2048]{2,1,0:T(8,128)(2,1)S(1)} %bitcast.156), channel_id=1, replica_groups=mesh['groups'=2,'seq'=16,'dp'=8] {'seq','dp'}, dimensions={0} | all-to-all | bytes 10485760 | tf_op jit(solution)/shard_map/all_to_all | solution.py:124
  389.1 11.9 %fusion.4 = f32[128,10,352]{0,2,1:T(8,128)} fusion(bf16[128,10,2048]{2,1,0:T(8,128)(2,1)} %all_to_all.69, bf16[1,2048,352]{1,2,0:T(8,128)(2,1)S(1)} %copy-done.13), kind=kOutput, calls=%fused_computation.11 | convolution fusion | flops 1845493760 | bytes 8486912 | tf_op jit(solution)/shard_map/npcd,pdf->npcf/dot_general | solution.py:42
  401.1 16.3 %convolution_convert_fusion = bf16[128,10,2048]{2,0,1:T(8,128)(2,1)} fusion(bf16[1,352,2048]{2,1,0:T(8,128)(2,1)S(1)} %copy-done, bf16[1,2048,352]{1,2,0:T(8,128)(2,1)} %param.24, bf16[128,10,2048]{2,1,0:T(8,128)(2,1)} %all_to_all.69, f32[128,10,352]{0,2,1:T(8,128)} %fusion.4), kind=kOutput, calls=%fused_computation.7 | convolution fusion | flops 3696312320 | bytes 15171584 | tf_op jit(solution)/shard_map/npcf,pfd->npcd/dot_general | solution.py:47
  417.4 9.2 %copy.85 = bf16[128,10,2048]{2,1,0:T(8,128)(2,1)} copy(bf16[128,10,2048]{2,0,1:T(8,128)(2,1)} %convolution_convert_fusion) | data formatting | bytes 10485760 | tf_op jit(solution)/shard_map/convert_element_type | solution.py:49
  426.6 12.0 %all-to-all-start.5 = ((bf16[128,10,2048]{2,1,0:T(8,128)(2,1)}), bf16[128,10,2048]{2,1,0:T(8,128)(2,1)}, u32[]{:S(2)}, u32[]{:S(2)}) async-start(bf16[128,10,2048]{2,1,0:T(8,128)(2,1)} %copy.85), calls=%async_computation.5 | async-start | bytes 16777216 | tf_op jit(solution)/shard_map/all_to_all | solution.py:134
  438.7 0.7 all-gather.5.cloned.1.call-update
  439.5 88.2 %all-gather.5.cloned.1.call-done = bf16[512,2048]{1,0:T(8,128)(2,1)} async-done(((bf16[64,2048]{1,0:T(8,128)(2,1)}), bf16[512,2048]{1,0:T(8,128)(2,1)}) %all-gather.5.cloned.1.call-update) | async-done | bytes 2097168 | tf_op jit(solution)/shard_map/all_gather | solution.py:105
  527.7 3.5 fusion.54
  531.3 5.6 convolution_convert_fusion.1
  537.3 0.1 copy.81
  537.5 0.7 copy.76
  538.3 0.2 fusion.26
  538.5 155.8 %all-to-all-done.5 = bf16[128,10,2048]{2,1,0:T(8,128)(2,1)} async-done(((bf16[128,10,2048]{2,1,0:T(8,128)(2,1)}), bf16[128,10,2048]{2,1,0:T(8,128)(2,1)}, u32[]{:S(2)}, u32[]{:S(2)}) %all-to-all-start.5) | async-done | bytes 5242912 | tf_op jit(solution)/shard_map/all_to_all | solution.py:134
  694.3 7.9 %convert_reduce_fusion = f32[32,10,2048]{2,1,0:T(8,128)} fusion(bf16[128,10,2048]{2,1,0:T(8,128)(2,1)} %all-to-all-done.5), kind=kLoop, calls=%fused_computation.1 | loop fusion | flops 4587520 | bytes 7864320 | tf_op jit(solution)/shard_map/reduce_sum | solution.py:141
  702.2 3.2 reshape.181
  705.4 2.7 gather_fusion
  708.1 2.0 gather.7
  710.1 3.9 multiply_reduce_fusion
  714.0 2.0 fusion.44
  (60 shorter events, 1.6 us)
Async XLA Ops:
  6.5 394.5 %copy-start = (bf16[1,352,2048]{2,1,0:T(8,128)(2,1)S(1)}, bf16[1,352,2048]{2,1,0:T(8,128)(2,1)}, u32[]{:S(2)}) copy-start(bf16[1,352,2048]{2,1,0:T(8,128)(2,1)} %param.25) | copy-start | bytes 4325380
  6.6 15.7 %copy-start.6 = (bf16[1,64,2048]{2,1,0:T(8,128)(2,1)S(1)}, bf16[1,64,2048]{2,1,0:T(8,128)(2,1)}, u32[]{:S(2)}) copy-start(bf16[1,64,2048]{2,1,0:T(8,128)(2,1)} %param.17) | copy-start | bytes 786436
  8.8 29.2 %all-to-all-start = ((bf16[2,64,16,1,128]{4,1,0,3,2:T(8,128)(2,1)}), bf16[2,64,16,1,128]{4,1,0,3,2:T(8,128)(2,1)S(1)}, u32[]{:S(2)}, u32[]{:S(2)}) async-start(bf16[2,64,16,1,128]{4,1,0,3,2:T(8,128)(2,1)} %copy.71), calls=%async_computation | async-start | bytes 1048576 | tf_op jit(solution)/shard_map/all_to_all | solution.py:84
  22.2 20.4 %copy-start.16 = (s32[1,1024]{1,0:T(1,128)S(1)}, s32[1,1024]{1,0:T(1,128)}, u32[]{:S(2)}) copy-start(s32[1,1024]{1,0:T(1,128)} %param.18) | copy-start | bytes 12292
  38.0 15.7 %all-to-all-start.1 = ((bf16[1,64,16,1,128]{4,1,3,0,2:T(8,128)(2,1)}), bf16[1,64,16,1,128]{4,1,3,0,2:T(8,128)(2,1)S(1)}, u32[]{:S(2)}, u32[]{:S(2)}) async-start(bf16[1,64,16,1,128]{4,1,3,0,2:T(8,128)(2,1)} %copy.73), calls=%async_computation.1 | async-start | bytes 524288 | tf_op jit(solution)/shard_map/all_to_all | solution.py:85
  42.4 76.7 %all-gather.3.cloned.1.call-start = ((), (), s32[]{:S(2)}) async-start(), calls=%async_computation.7 | async-start | bytes 2359296 | tf_op jit(solution)/shard_map/all_gather | solution.py:94
  43.6 1.9 copy-start.2
  53.7 18.3 %copy-start.8 = (s32[1,64,4]{1,2,0:T(4,128)S(1)}, s32[1,64,4]{1,2,0:T(4,128)}, u32[]{:S(2)}) copy-start(s32[1,64,4]{1,2,0:T(4,128)} %param.21) | copy-start | bytes 3076
  53.7 65.5 %copy-start.15 = (bf16[2048,256]{1,0:T(8,128)(2,1)S(1)}, bf16[2048,256]{1,0:T(8,128)(2,1)}, u32[]{:S(2)}) copy-start(bf16[2048,256]{1,0:T(8,128)(2,1)} %param.19) | copy-start | bytes 3145732
  122.2 12.6 %copy-start.7 = (bf16[1,64,2048]{2,1,0:T(8,128)(2,1)S(1)}, bf16[1,64,2048]{2,1,0:T(8,128)(2,1)}, u32[]{:S(2)}) copy-start(bf16[1,64,2048]{2,1,0:T(8,128)(2,1)} %param.15) | copy-start | bytes 786436
  122.2 13.5 %copy-start.9 = (f32[2048]{0:T(1024)S(1)}, f32[2048]{0:T(1024)}, u32[]{:S(2)}) copy-start(f32[2048]{0:T(1024)} %param.20) | copy-start | bytes 24580
  122.2 12.5 %all-to-all-start.3 = ((bf16[8,64,256]{2,1,0:T(8,128)(2,1)}), bf16[8,64,256]{2,1,0:T(8,128)(2,1)S(1)}, u32[]{:S(2)}, u32[]{:S(2)}) async-start(bf16[8,64,256]{2,1,0:T(8,128)(2,1)} %bitcast.16), calls=%async_computation.3 | async-start | bytes 524288 | tf_op jit(solution)/shard_map/all_to_all | solution.py:98
  134.9 0.7 copy-start.3
  135.8 0.7 copy-start.4
  141.5 247.7 %copy-start.13 = (bf16[1,2048,352]{1,2,0:T(8,128)(2,1)S(1)}, bf16[1,2048,352]{1,2,0:T(8,128)(2,1)}, u32[]{:S(2)}) copy-start(bf16[1,2048,352]{1,2,0:T(8,128)(2,1)} %param.23) | copy-start | bytes 4325380
  426.6 101.1 %copy-start.14 = (bf16[2048,352]{0,1:T(8,128)(2,1)S(1)}, bf16[2048,352]{0,1:T(8,128)(2,1)}, u32[]{:S(2)}) copy-start(bf16[2048,352]{0,1:T(8,128)(2,1)} %param.26) | copy-start | bytes 4325380
  426.6 267.6 %all-to-all-start.5 = ((bf16[128,10,2048]{2,1,0:T(8,128)(2,1)}), bf16[128,10,2048]{2,1,0:T(8,128)(2,1)}, u32[]{:S(2)}, u32[]{:S(2)}) async-start(bf16[128,10,2048]{2,1,0:T(8,128)(2,1)} %copy.85), calls=%async_computation.5 | async-start | bytes 16777216 | tf_op jit(solution)/shard_map/all_to_all | solution.py:134
  438.6 89.1 %all-gather.5.cloned.1.call-start = ((), (), s32[]{:S(2)}) async-start(), calls=%async_computation.8 | async-start | bytes 2359296 | tf_op jit(solution)/shard_map/all_gather | solution.py:105
  439.4 274.6 %reduce-scatter.2.cloned.1.call-start = ((), (), s32[]{:S(2)}) async-start(), calls=%async_computation.9 | async-start | bytes 2359296 | tf_op jit(solution)/shard_map/reduce_scatter | solution.py:107
  527.7 3.6 copy-start.12
  536.8 0.7 copy-start.11
  536.9 1.4 copy-start.10
  536.9 1.4 copy-start.5
  708.1 7.9 %copy-start.1 = (bf16[1,352,2048]{2,1,0:T(8,128)(2,1)S(1)}, bf16[1,352,2048]{2,1,0:T(8,128)(2,1)}, u32[]{:S(2)}) copy-start(bf16[1,352,2048]{2,1,0:T(8,128)(2,1)} %param.25) | copy-start | bytes 4325380
Sparse Core Ops, SparseCore 0:
  72.1 47.0 all-gather.2
  441.3 86.4 all-gather.4
  537.0 109.4 reduce-scatter.1
where the time goes:
time: 732 us; the launch traced here: 723 us
  waiting for transfers between devices  318 us (43%)
  blocking collectives  262 us (36%)
  matrix products  46.3 us (6%)
  starting transfers between devices  37.4 us (5%)
  local copies, waits for them, and re-layouts  29.9 us (4%)
  other arithmetic  15.7 us (2%)
  between operations  13.9 us (2%)
    all_to_all x1, blocking collectives, body(): lax.all_to_all(outgoing.reshape(EXPERTS * SPLIT, CAP, model_width), ('seq...  248 us
    all_to_all x1, waiting for transfers between devices, body(): lax.all_to_all(results.reshape(devices * own_pieces, CAP, model_width), (...  156 us
    all_gather x1, waiting for transfers between devices, body(): lax.all_gather(normed, 'dp', axis=0, tiled=True)  88.2 us
    all_gather x1, waiting for transfers between devices, body(): lax.all_gather(own_attended, 'dp', axis=0, tiled=True)  46.4 us
    dot_general x1, matrix products, piece_block(): jnp.einsum('npcf,pfd->npcd', hidden, down_matrix, preferred_element_type=...  16.3 us
    all_to_all x1, waiting for transfers between devices, body(): lax.all_to_all(paired, 'seq', split_axis=2, concat_axis=1, tiled=True)  14.9 us
  transfers between devices with their start and end apart: 7, of which 6 were waited for; matrix products, arithmetic and copies ran while one was open for 5% of the time, Pallas kernels for 0%

commit v1 on v0

--- a/solution.py
+++ b/solution.py
@@ -10,6 +10,24 @@
 SPLIT = 4
 CAP = 10
 norm_eps = 1e-06
+
+
+def collect(array, axis, dim):
+    ways, here, hop = (lax.axis_size(axis), lax.axis_index(axis), array.shape[dim])
+    shape = [n * ways if d == dim else n for d, n in enumerate(array.shape)]
+    full = lax.dynamic_update_slice_in_dim(
+        jnp.zeros(shape, array.dtype), array, here * hop, axis=dim
+    )
+    going_up = going_down = array
+    for far in range(1, ways // 2 + 1):
+        going_up = lax.ppermute(going_up, axis, [(d, (d + 1) % ways) for d in range(ways)])
+        full = lax.dynamic_update_slice_in_dim(full, going_up, (here - far) % ways * hop, axis=dim)
+        if 2 * far < ways:
+            going_down = lax.ppermute(going_down, axis, [(d, (d - 1) % ways) for d in range(ways)])
+            full = lax.dynamic_update_slice_in_dim(
+                full, going_down, (here + far) % ways * hop, axis=dim
+            )
+    return full
 
 
 def slot_numbers(routes):
@@ -91,9 +109,7 @@
         by_position, "seq", split_axis=0, concat_axis=2, tiled=True
     ).reshape(tokens, model_width)
     column_block = jnp.dot(
-        lax.all_gather(own_attended, "dp", axis=0, tiled=True),
-        out_weight,
-        preferred_element_type=jnp.float32,
+        collect(own_attended, "dp", 0), out_weight, preferred_element_type=jnp.float32
     ).astype(jnp.bfloat16)
     projected = lax.all_to_all(column_block, "dp", split_axis=0, concat_axis=1, tiled=True)
     residual = (resid[0].astype(jnp.float32) + projected.astype(jnp.float32)).astype(jnp.bfloat16)

time: 732 us -> 691 us (0.944)
  the two profiles are of different devices: /device:TPU:520 before, /device:TPU:522 now
where the time goes in v1:
time: 691 us; the launch traced here: 682 us
  waiting for transfers between devices  306 us (44%)
  blocking collectives  205 us (30%)
  starting transfers between devices  66 us (10%)
  matrix products  45.5 us (7%)
  local copies, waits for them, and re-layouts  30 us (4%)
  other arithmetic  15.7 us (2%)
  between operations  14.1 us (2%)
    all_to_all x1, blocking collectives, body(): lax.all_to_all(outgoing.reshape(EXPERTS * SPLIT, CAP, model_width), ('seq...  205 us
    all_to_all x1, waiting for transfers between devices, body(): lax.all_to_all(results.reshape(devices * own_pieces, CAP, model_width), (...  154 us
    all_gather x1, waiting for transfers between devices, body(): lax.all_gather(normed, 'dp', axis=0, tiled=True)  91.6 us
    ppermute x4, waiting for transfers between devices, collect(): lax.ppermute(going_up, axis, [(d, (d + 1) % ways) for d in range(ways)])  19.2 us
    all_to_all x1, starting transfers between devices, body(): lax.all_to_all(results.reshape(devices * own_pieces, CAP, model_width), (...  17.9 us
    dot_general x1, matrix products, piece_block(): jnp.einsum('npcf,pfd->npcd', hidden, down_matrix, preferred_element_type=...  16.3 us
    all_to_all x1, waiting for transfers between devices, body(): lax.all_to_all(paired, 'seq', split_axis=2, concat_axis=1, tiled=True)  14.9 us
  transfers between devices with their start and end apart: 14, of which 13 were waited for; matrix products, arithmetic and copies ran while one was open for 5% of the time, Pallas kernels for 0%

profile of v1, /device:TPU:522, one launch (start us, length us, event | category | flops | bytes accessed | tf_op | source)
XLA Modules:
  0.0 681.9 jit_solution(11233820124317710154)
XLA Ops:
  6.6 1.3 copy.92
  7.8 0.9 copy.71
  8.8 13.5 %all-to-all-start = ((bf16[2,64,16,1,128]{4,1,0,3,2:T(8,128)(2,1)}), bf16[2,64,16,1,128]{4,1,0,3,2:T(8,128)(2,1)S(1)}, u32[]{:S(2)}, u32[]{:S(2)}) async-start(bf16[2,64,16,1,128]{4,1,0,3,2:T(8,128)(2,1)} %copy.71), calls=%async_computation | async-start | bytes 1048576 | tf_op jit(solution)/shard_map/all_to_all | solution.py:102
  22.3 0.8 copy.73
  23.1 14.9 %all-to-all-done = bf16[2,64,16,1,128]{4,1,0,3,2:T(8,128)(2,1)S(1)} async-done(((bf16[2,64,16,1,128]{4,1,0,3,2:T(8,128)(2,1)}), bf16[2,64,16,1,128]{4,1,0,3,2:T(8,128)(2,1)S(1)}, u32[]{:S(2)}, u32[]{:S(2)}) %all-to-all-start) | async-done | bytes 524320 | tf_op jit(solution)/shard_map/all_to_all | solution.py:102
  38.0 4.5 all-to-all-start.1
  42.5 1.0 fusion.53
  43.6 1.9 copy-done.2
  46.2 7.5 %all-to-all-done.1 = bf16[1,64,16,1,128]{4,1,3,0,2:T(8,128)(2,1)S(1)} async-done(((bf16[1,64,16,1,128]{4,1,3,0,2:T(8,128)(2,1)}), bf16[1,64,16,1,128]{4,1,3,0,2:T(8,128)(2,1)S(1)}, u32[]{:S(2)}, u32[]{:S(2)}) %all-to-all-start.1) | async-done | bytes 262176 | tf_op jit(solution)/shard_map/all_to_all | solution.py:103
  53.7 3.8 fusion.22
  57.4 4.0 all-to-all-start.2
  62.4 9.6 %all-to-all-done.2 = bf16[16,64,128]{2,1,0:T(8,128)(2,1)S(1)} async-done(((bf16[16,64,128]{2,1,0:T(8,128)(2,1)}), bf16[16,64,128]{2,1,0:T(8,128)(2,1)S(1)}, u32[]{:S(2)}, u32[]{:S(2)}) %all-to-all-start.2) | async-done | bytes 262176 | tf_op jit(solution)/shard_map/all_to_all | solution.py:108
  72.3 0.8 collective-permute-start
  73.1 1.3 collective-permute-start.1
  74.7 6.6 collective-permute-done
  81.3 0.7 collective-permute-start.2
  82.3 1.5 collective-permute-start.3
  83.9 6.5 collective-permute-done.2
  90.4 4.8 collective-permute-start.4
  95.2 1.2 collective-permute-done.3
  96.4 4.0 collective-permute-done.4
  100.4 3.2 collective-permute-start.6
  103.6 1.9 collective-permute-done.5
  105.6 2.2 collective-permute-done.6
  107.8 1.4 convolution_convert_fusion.3
  109.2 13.7 %all-to-all-start.3 = ((bf16[8,64,256]{2,1,0:T(8,128)(2,1)}), bf16[8,64,256]{2,1,0:T(8,128)(2,1)S(1)}, u32[]{:S(2)}, u32[]{:S(2)}) async-start(bf16[8,64,256]{2,1,0:T(8,128)(2,1)} %bitcast.16), calls=%async_computation.3 | async-start | bytes 524288 | tf_op jit(solution)/shard_map/all_to_all | solution.py:114
  123.6 4.5 all-to-all-done.3
  128.4 0.7 copy-done.3
  130.0 1.6 convolution_convert_fusion.2
  131.6 2.3 broadcast_in_dim.40
  133.9 1.1 broadcast_in_dim.41
  135.0 205.0 %all_to_all.68 = bf16[128,10,2048]{2,1,0:T(8,128)(2,1)} all-to-all(bf16[128,10,2048]{2,1,0:T(8,128)(2,1)S(1)} %bitcast.158), channel_id=1, replica_groups=mesh['groups'=2,'seq'=16,'dp'=8] {'seq','dp'}, dimensions={0} | all-to-all | bytes 10485760 | tf_op jit(solution)/shard_map/all_to_all | solution.py:140
  340.0 12.1 %fusion.4 = f32[128,10,352]{0,2,1:T(8,128)} fusion(bf16[128,10,2048]{2,1,0:T(8,128)(2,1)} %all_to_all.68, bf16[1,2048,352]{1,2,0:T(8,128)(2,1)S(1)} %copy-done.13), kind=kOutput, calls=%fused_computation.11 | convolution fusion | flops 1845493760 | bytes 8486912 | tf_op jit(solution)/shard_map/npcd,pdf->npcf/dot_general | solution.py:60
  352.1 16.3 %convolution_convert_fusion = bf16[128,10,2048]{2,0,1:T(8,128)(2,1)} fusion(bf16[1,352,2048]{2,1,0:T(8,128)(2,1)S(1)} %copy-done, bf16[1,2048,352]{1,2,0:T(8,128)(2,1)} %param.24, bf16[128,10,2048]{2,1,0:T(8,128)(2,1)} %all_to_all.68, f32[128,10,352]{0,2,1:T(8,128)} %fusion.4), kind=kOutput, calls=%fused_computation.7 | convolution fusion | flops 3696312320 | bytes 15171584 | tf_op jit(solution)/shard_map/npcf,pfd->npcd/dot_general | solution.py:65
  368.5 9.3 %copy.85 = bf16[128,10,2048]{2,1,0:T(8,128)(2,1)} copy(bf16[128,10,2048]{2,0,1:T(8,128)(2,1)} %convolution_convert_fusion) | data formatting | bytes 10485760 | tf_op jit(solution)/shard_map/convert_element_type | solution.py:67
  377.8 17.9 %all-to-all-start.5 = ((bf16[128,10,2048]{2,1,0:T(8,128)(2,1)}), bf16[128,10,2048]{2,1,0:T(8,128)(2,1)}, u32[]{:S(2)}, u32[]{:S(2)}) async-start(bf16[128,10,2048]{2,1,0:T(8,128)(2,1)} %copy.85), calls=%async_computation.5 | async-start | bytes 16777216 | tf_op jit(solution)/shard_map/all_to_all | solution.py:150
  395.8 0.7 all-gather.2.cloned.1.call-update
  396.6 91.6 %all-gather.2.cloned.1.call-done = bf16[512,2048]{1,0:T(8,128)(2,1)} async-done(((bf16[64,2048]{1,0:T(8,128)(2,1)}), bf16[512,2048]{1,0:T(8,128)(2,1)}) %all-gather.2.cloned.1.call-update) | async-done | bytes 2097168 | tf_op jit(solution)/shard_map/all_gather | solution.py:121
  488.3 3.6 fusion.54
  491.8 5.6 convolution_convert_fusion.1
  498.1 0.7 copy.76
  499.0 154.0 %all-to-all-done.5 = bf16[128,10,2048]{2,1,0:T(8,128)(2,1)} async-done(((bf16[128,10,2048]{2,1,0:T(8,128)(2,1)}), bf16[128,10,2048]{2,1,0:T(8,128)(2,1)}, u32[]{:S(2)}, u32[]{:S(2)}) %all-to-all-start.5) | async-done | bytes 5242912 | tf_op jit(solution)/shard_map/all_to_all | solution.py:150
  653.0 7.9 %convert_reduce_fusion = f32[32,10,2048]{2,1,0:T(8,128)} fusion(bf16[128,10,2048]{2,1,0:T(8,128)(2,1)} %all-to-all-done.5), kind=kLoop, calls=%fused_computation.1 | loop fusion | flops 4587520 | bytes 7864320 | tf_op jit(solution)/shard_map/reduce_sum | solution.py:157
  660.9 3.4 reshape.181
  664.3 2.7 gather_fusion
  667.0 2.0 gather.7
  669.0 3.9 multiply_reduce_fusion
  672.9 2.0 fusion.44
  (81 shorter events, 5.3 us)
Async XLA Ops:
  6.5 345.6 %copy-start = (bf16[1,352,2048]{2,1,0:T(8,128)(2,1)S(1)}, bf16[1,352,2048]{2,1,0:T(8,128)(2,1)}, u32[]{:S(2)}) copy-start(bf16[1,352,2048]{2,1,0:T(8,128)(2,1)} %param.25) | copy-start | bytes 4325380
  6.6 15.7 %copy-start.6 = (bf16[1,64,2048]{2,1,0:T(8,128)(2,1)S(1)}, bf16[1,64,2048]{2,1,0:T(8,128)(2,1)}, u32[]{:S(2)}) copy-start(bf16[1,64,2048]{2,1,0:T(8,128)(2,1)} %param.17) | copy-start | bytes 786436
  8.8 29.2 %all-to-all-start = ((bf16[2,64,16,1,128]{4,1,0,3,2:T(8,128)(2,1)}), bf16[2,64,16,1,128]{4,1,0,3,2:T(8,128)(2,1)S(1)}, u32[]{:S(2)}, u32[]{:S(2)}) async-start(bf16[2,64,16,1,128]{4,1,0,3,2:T(8,128)(2,1)} %copy.71), calls=%async_computation | async-start | bytes 1048576 | tf_op jit(solution)/shard_map/all_to_all | solution.py:102
  22.2 20.3 %copy-start.16 = (s32[1,1024]{1,0:T(1,128)S(1)}, s32[1,1024]{1,0:T(1,128)}, u32[]{:S(2)}) copy-start(s32[1,1024]{1,0:T(1,128)} %param.18) | copy-start | bytes 12292
  38.0 15.7 %all-to-all-start.1 = ((bf16[1,64,16,1,128]{4,1,3,0,2:T(8,128)(2,1)}), bf16[1,64,16,1,128]{4,1,3,0,2:T(8,128)(2,1)S(1)}, u32[]{:S(2)}, u32[]{:S(2)}) async-start(bf16[1,64,16,1,128]{4,1,3,0,2:T(8,128)(2,1)} %copy.73), calls=%async_computation.1 | async-start | bytes 524288 | tf_op jit(solution)/shard_map/all_to_all | solution.py:103
  43.6 2.0 copy-start.2
  53.7 7.9 %copy-start.8 = (s32[1,64,4]{1,2,0:T(4,128)S(1)}, s32[1,64,4]{1,2,0:T(4,128)}, u32[]{:S(2)}) copy-start(s32[1,64,4]{1,2,0:T(4,128)} %param.21) | copy-start | bytes 3076
  57.4 14.6 %all-to-all-start.2 = ((bf16[16,64,128]{2,1,0:T(8,128)(2,1)}), bf16[16,64,128]{2,1,0:T(8,128)(2,1)S(1)}, u32[]{:S(2)}, u32[]{:S(2)}) async-start(bf16[16,64,128]{2,1,0:T(8,128)(2,1)} %bitcast.13), calls=%async_computation.2 | async-start | bytes 524288 | tf_op jit(solution)/shard_map/all_to_all | solution.py:108
  72.3 9.0 %collective-permute-start = (bf16[64,2048]{1,0:T(8,128)(2,1)S(1)}, bf16[64,2048]{1,0:T(8,128)(2,1)S(1)}, u32[]{:S(2)}, u32[]{:S(2)}) collective-permute-start(bf16[64,2048]{1,0:T(8,128)(2,1)S(1)} %bitcast.169), channel_id=1, source_target_pairs={{0,1},{1,2},{2,3},{3,4},{4,5},{5,6},{6,7},{7,0},{8,9},{9,10},{10,1... | collective-permute-start | bytes 786440 | tf_op jit(solution)/shard_map/ppermute | solution.py:23
  73.1 9.2 %collective-permute-start.1 = (bf16[64,2048]{1,0:T(8,128)(2,1)S(1)}, bf16[64,2048]{1,0:T(8,128)(2,1)S(1)}, u32[]{:S(2)}, u32[]{:S(2)}) collective-permute-start(bf16[64,2048]{1,0:T(8,128)(2,1)S(1)} %bitcast.170), channel_id=1, source_target_pairs={{0,7},{1,0},{2,1},{3,2},{4,3},{5,4},{6,5},{7,6},{8,15},{9,8},{10,9... | collective-permute-start | bytes 786440 | tf_op jit(solution)/shard_map/ppermute | solution.py:26
  74.7 33.1 %copy-start.15 = (bf16[2048,256]{1,0:T(8,128)(2,1)S(1)}, bf16[2048,256]{1,0:T(8,128)(2,1)}, u32[]{:S(2)}) copy-start(bf16[2048,256]{1,0:T(8,128)(2,1)} %param.19) | copy-start | bytes 3145732
  81.3 9.1 %collective-permute-start.2 = (bf16[64,2048]{1,0:T(8,128)(2,1)S(1)}, bf16[64,2048]{1,0:T(8,128)(2,1)S(1)}, u32[]{:S(2)}, u32[]{:S(2)}) collective-permute-start(bf16[64,2048]{1,0:T(8,128)(2,1)S(1)} %collective-permute-done), channel_id=1, source_target_pairs={{0,1},{1,2},{2,3},{3,4},{4,5},{5,6},{6,7},{7,0},{8,9},{9,10},{10,1... | collective-permute-start | bytes 786440 | tf_op jit(solution)/shard_map/ppermute | solution.py:23
  82.3 14.1 %collective-permute-start.3 = (bf16[64,2048]{1,0:T(8,128)(2,1)S(1)}, bf16[64,2048]{1,0:T(8,128)(2,1)S(1)}, u32[]{:S(2)}, u32[]{:S(2)}) collective-permute-start(bf16[64,2048]{1,0:T(8,128)(2,1)S(1)} %collective-permute-done.1), channel_id=1, source_target_pairs={{0,7},{1,0},{2,1},{3,2},{4,3},{5,4},{6,5},{7,6},{8,15},{9,8},{10,9... | collective-permute-start | bytes 786440 | tf_op jit(solution)/shard_map/ppermute | solution.py:26
  90.4 10.0 %collective-permute-start.4 = (bf16[64,2048]{1,0:T(8,128)(2,1)S(1)}, bf16[64,2048]{1,0:T(8,128)(2,1)S(1)}, u32[]{:S(2)}, u32[]{:S(2)}) collective-permute-start(bf16[64,2048]{1,0:T(8,128)(2,1)S(1)} %collective-permute-done.2), channel_id=1, source_target_pairs={{0,1},{1,2},{2,3},{3,4},{4,5},{5,6},{6,7},{7,0},{8,9},{9,10},{10,1... | collective-permute-start | bytes 786440 | tf_op jit(solution)/shard_map/ppermute | solution.py:23
  96.4 9.2 %collective-permute-start.5 = (bf16[64,2048]{1,0:T(8,128)(2,1)S(1)}, bf16[64,2048]{1,0:T(8,128)(2,1)S(1)}, u32[]{:S(2)}, u32[]{:S(2)}) collective-permute-start(bf16[64,2048]{1,0:T(8,128)(2,1)S(1)} %collective-permute-done.3), channel_id=1, source_target_pairs={{0,7},{1,0},{2,1},{3,2},{4,3},{5,4},{6,5},{7,6},{8,15},{9,8},{10,9... | collective-permute-start | bytes 786440 | tf_op jit(solution)/shard_map/ppermute | solution.py:26
  100.4 7.3 %collective-permute-start.6 = (bf16[64,2048]{1,0:T(8,128)(2,1)S(1)}, bf16[64,2048]{1,0:T(8,128)(2,1)S(1)}, u32[]{:S(2)}, u32[]{:S(2)}) collective-permute-start(bf16[64,2048]{1,0:T(8,128)(2,1)S(1)} %collective-permute-done.4), channel_id=1, source_target_pairs={{0,1},{1,2},{2,3},{3,4},{4,5},{5,6},{6,7},{7,0},{8,9},{9,10},{10,1... | collective-permute-start | bytes 786440 | tf_op jit(solution)/shard_map/ppermute | solution.py:23
  109.2 19.0 %copy-start.7 = (bf16[1,64,2048]{2,1,0:T(8,128)(2,1)S(1)}, bf16[1,64,2048]{2,1,0:T(8,128)(2,1)}, u32[]{:S(2)}) copy-start(bf16[1,64,2048]{2,1,0:T(8,128)(2,1)} %param.15) | copy-start | bytes 786436
  109.2 19.9 %copy-start.9 = (f32[2048]{0:T(1024)S(1)}, f32[2048]{0:T(1024)}, u32[]{:S(2)}) copy-start(f32[2048]{0:T(1024)} %param.20) | copy-start | bytes 24580
  109.2 19.0 %all-to-all-start.3 = ((bf16[8,64,256]{2,1,0:T(8,128)(2,1)}), bf16[8,64,256]{2,1,0:T(8,128)(2,1)S(1)}, u32[]{:S(2)}, u32[]{:S(2)}) async-start(bf16[8,64,256]{2,1,0:T(8,128)(2,1)} %bitcast.16), calls=%async_computation.3 | async-start | bytes 524288 | tf_op jit(solution)/shard_map/all_to_all | solution.py:114
  128.4 0.7 copy-start.3
  129.3 0.7 copy-start.4
  135.0 205.0 %copy-start.13 = (bf16[1,2048,352]{1,2,0:T(8,128)(2,1)S(1)}, bf16[1,2048,352]{1,2,0:T(8,128)(2,1)}, u32[]{:S(2)}) copy-start(bf16[1,2048,352]{1,2,0:T(8,128)(2,1)} %param.23) | copy-start | bytes 4325380
  377.8 110.4 %copy-start.14 = (bf16[2048,352]{0,1:T(8,128)(2,1)S(1)}, bf16[2048,352]{0,1:T(8,128)(2,1)}, u32[]{:S(2)}) copy-start(bf16[2048,352]{0,1:T(8,128)(2,1)} %param.26) | copy-start | bytes 4325380
  377.8 275.1 %all-to-all-start.5 = ((bf16[128,10,2048]{2,1,0:T(8,128)(2,1)}), bf16[128,10,2048]{2,1,0:T(8,128)(2,1)}, u32[]{:S(2)}, u32[]{:S(2)}) async-start(bf16[128,10,2048]{2,1,0:T(8,128)(2,1)} %copy.85), calls=%async_computation.5 | async-start | bytes 16777216 | tf_op jit(solution)/shard_map/all_to_all | solution.py:150
  395.8 92.5 %all-gather.2.cloned.1.call-start = ((), (), s32[]{:S(2)}) async-start(), calls=%async_computation.7 | async-start | bytes 2359296 | tf_op jit(solution)/shard_map/all_gather | solution.py:121
  396.6 276.4 %reduce-scatter.2.cloned.1.call-start = ((), (), s32[]{:S(2)}) async-start(), calls=%async_computation.8 | async-start | bytes 2359296 | tf_op jit(solution)/shard_map/reduce_scatter | solution.py:123
  488.3 3.6 copy-start.12
  497.4 0.7 copy-start.11
  497.4 1.4 copy-start.10
  497.4 1.4 copy-start.5
  667.0 7.9 %copy-start.1 = (bf16[1,352,2048]{2,1,0:T(8,128)(2,1)S(1)}, bf16[1,352,2048]{2,1,0:T(8,128)(2,1)}, u32[]{:S(2)}) copy-start(bf16[1,352,2048]{2,1,0:T(8,128)(2,1)} %param.25) | copy-start | bytes 4325380
Sparse Core Ops, SparseCore 0:
  398.4 89.8 all-gather.1
  497.6 109.6 reduce-scatter.1
